TPU v7x, 32 devices: a whole 2x2x4 slice. The times are simulated.
32 devices in a mesh: row: 4 (over y, x), col: 2 (over core), layer: 4 (over z).
Axes of the slice: x: 2, y: 2, z: 4, core: 2. Of those that a mesh axis runs over, the one named last changes fastest.
Arguments:
- matrix: float32 [4096, 4096], P('row', 'col'), may hold values from -6 to 6
- pattern: int32 [128, 128], P('row', 'col'), may hold values 0 or 1
- keep: int32 [128, 128], P('row', 'col'), may hold values 0 or 1
Outputs:
- update: float32 [4096, 4096], P(('row', 'layer'), 'col')
All inputs are finite; a program needn't handle non-finite values. No bound on the sum of `pattern` or of `keep` on one device may be relied on, other than what follows from the above.
Results may differ from a plain program's by a relative error of at most 0.00005.
Values sent between devices are 32-bit elements; how exact they have to be, the bound alone decides.
A program may use at most 128 MiB of HBM per device.

v0:
```python
import jax
import jax.numpy as jnp
from jax import lax
from jax.sharding import PartitionSpec as P

BS = 32
NB = 128


def layer_rows(values, layers, level):
    count, width = values.shape
    shaped = values.reshape(count // (layers * BS), layers, BS, width)
    picked = lax.dynamic_index_in_dim(shaped, level, 1, keepdims=False)
    return picked.reshape(count // layers, width)


def local(matrix, pattern, keep):
    rows, cols = matrix.shape
    block_rows, block_cols = pattern.shape
    layers = lax.axis_size("layer")
    level = lax.axis_index("layer")
    sparse = (
        matrix.reshape(block_rows, BS, block_cols, BS)
        * pattern.astype(jnp.float32)[:, None, :, None]
    ).reshape(rows, cols)
    left_local = lax.dynamic_index_in_dim(
        sparse.reshape(rows, block_cols // layers, layers, BS), level, 2, keepdims=False
    )
    left_local = left_local.reshape(rows, block_cols // layers * BS)
    left_full = lax.all_gather(left_local, "col", axis=1, tiled=True)
    right_full = lax.all_gather(layer_rows(sparse, layers, level), "row", axis=0, tiled=True)
    partial_value = jnp.dot(
        left_full, right_full, preferred_element_type=jnp.float32, precision=lax.Precision.HIGHEST
    )
    keep_flags = keep.astype(jnp.float32)
    keep_mine = lax.dynamic_index_in_dim(
        keep_flags.reshape(block_rows // layers, layers, block_cols), level, 1, keepdims=False
    )
    square = lax.psum(partial_value, "layer")
    mine = layer_rows(square, layers, level)
    filtered = (
        mine.reshape(block_rows // layers, BS, block_cols, BS) * keep_mine[:, None, :, None]
    ).reshape(rows // layers, cols)
    filtered_full = lax.all_gather(filtered, "row", axis=0, tiled=True)
    share = rows // layers
    summed = lax.psum_scatter(
        jnp.dot(
            left_full,
            filtered_full,
            preferred_element_type=jnp.float32,
            precision=lax.Precision.HIGHEST,
        ),
        "layer",
        scatter_dimension=0,
        tiled=True,
    )
    own_rows = lax.dynamic_slice_in_dim(sparse, level * share, share, 0)
    factor = 0.72 / (NB * BS)
    return 1.5 * own_rows - 0.5 * factor * summed


def solution(mesh):
    placed = (P("row", "col"), P("row", "col"), P("row", "col"))
    return jax.shard_map(
        local, mesh=mesh, in_specs=placed, out_specs=P(("row", "layer"), "col"), check_vma=False
    )
```

profile of v0, /device:TPU:0, one launch (start us, length us, event | category | flops | bytes accessed | tf_op | source)
XLA Modules:
  0.0 727.2 jit_solution(3081529053856967968)
XLA Ops:
  6.5 0.7 convert_element_type.6
  7.3 9.3 %copy.4 = f32[1024,2048]{0,1:T(8,128)} copy(f32[1024,2048]{1,0:T(8,128)} %param.3) | data formatting | bytes 16777216 | tf_op args[0]
  16.6 0.3 mul.63
  16.9 0.5 mul.64
  17.5 3.3 dynamic-slice_multiply_fusion.1
  20.9 0.3 mul.67
  21.2 0.5 mul.68
  21.8 3.2 dynamic-slice_multiply_fusion
  25.1 12.3 %all-gather.4.cloned.1.call-done = f32[1024,1024]{0,1:T(8,128)} async-done(((f32[1024,512]{0,1:T(8,128)}), f32[1024,1024]{0,1:T(8,128)}) %all-gather.4.cloned.1.call-update) | async-done | bytes 4194320 | tf_op jit(solution)/shard_map/all_gather | solution.py:30
  37.4 90.5 %all-gather.6.cloned.1.call-done = f32[1024,2048]{1,0:T(8,128)} async-done(((f32[256,2048]{1,0:T(8,128)}), f32[1024,2048]{1,0:T(8,128)}) %all-gather.6.cloned.1.call-update) | async-done | bytes 8388624 | tf_op jit(solution)/shard_map/all_gather | solution.py:31
  127.9 31.0 %fusion.2 = f32[1024,2048]{1,0:T(8,128)} fusion(f32[1024,1024]{0,1:T(8,128)} %all-gather.4.cloned.1.call-done, f32[1024,2048]{1,0:T(8,128)} %all-gather.6.cloned.1.call-done), kind=kOutput, calls=%fused_computation.10 | convolution fusion | flops 25769803776 | bytes 20971520 | tf_op jit(solution)/shard_map/dot_general | solution.py:32
  159.0 0.6 copy-done
  159.7 4.4 mul.72
  164.0 6.9 mul.73
  170.9 279.0 %all-reduce.2.cloned.1.call-done = f32[8,4,32,2048]{3,2,1,0:T(8,128)} async-done(((f32[8,4,32,2048]{3,2,1,0:T(8,128)}), f32[8,4,32,2048]{3,2,1,0:T(8,128)}) %all-reduce.2.cloned.1.call-update) | async-done | bytes 8388624 | tf_op jit(solution)/shard_map/psum | solution.py:39
  449.9 1.7 constant_dynamic-slice_fusion.1
  451.7 1.6 bitcast_multiply_fusion
  453.3 0.2 reduce-scatter.2.cloned.1.call-start
  453.5 86.4 %all-gather.8.cloned.1.call-done = f32[1024,2048]{1,0:T(8,128)} async-done(((f32[256,2048]{1,0:T(8,128)}), f32[1024,2048]{1,0:T(8,128)}) %all-gather.8.cloned.1.call-update) | async-done | bytes 8388624 | tf_op jit(solution)/shard_map/all_gather | solution.py:44
  539.9 31.0 %fusion.3 = f32[1024,2048]{1,0:T(8,128)} fusion(f32[1024,1024]{0,1:T(8,128)} %all-gather.4.cloned.1.call-done, f32[1024,2048]{1,0:T(8,128)} %all-gather.8.cloned.1.call-done), kind=kOutput, calls=%fused_computation.11 | convolution fusion | flops 25769803776 | bytes 20971520 | tf_op jit(solution)/shard_map/dot_general | solution.py:47
  571.0 11.7 %mul.57 = f32[32,32,64,32]{3,2,1,0:T(8,128)} broadcast(f32[32,64]{1,0:T(8,128)S(1)} %convert_element_type.6), dimensions={0,2} | broadcast | bytes 8396800 | tf_op jit(solution)/shard_map/mul | solution.py:23
  582.6 25.5 %mul.58 = f32[1024,2048]{1,0:T(8,128)} reshape(f32[32,32,64,32]{3,2,1,0:T(8,128)} %mul.57) | data formatting | bytes 16777216 | tf_op jit(solution)/shard_map/mul | solution.py:23
  608.1 107.7 %reduce-scatter.2.cloned.1.call-done = f32[256,2048]{1,0:T(8,128)} async-done(((f32[1024,2048]{1,0:T(8,128)}), f32[256,2048]{1,0:T(8,128)}) %reduce-scatter.2.cloned.1.call-update) | async-done | bytes 2097168 | tf_op jit(solution)/shard_map/reduce_scatter | solution.py:46
  715.7 5.0 fusion.1
  (15 shorter events, 0.4 us)
Async XLA Ops:
  6.5 30.8 %all-gather.4.cloned.1.call-start = ((), (), s32[]{:S(2)}) async-start(), calls=%async_computation.1 | async-start | bytes 6291456 | tf_op jit(solution)/shard_map/all_gather | solution.py:30
  20.8 107.1 %all-gather.6.cloned.1.call-start = ((), (), s32[]{:S(2)}) async-start(), calls=%async_computation.2 | async-start | bytes 10485760 | tf_op jit(solution)/shard_map/all_gather | solution.py:31
  25.0 424.9 %all-reduce.2.cloned.1.call-start = ((), (), s32[]{:S(2)}) async-start(), calls=%async_computation.3 | async-start | bytes 16777216 | tf_op jit(solution)/shard_map/psum | solution.py:39
  158.9 0.7 copy-start
  159.0 381.0 %all-gather.8.cloned.1.call-start = ((), (), s32[]{:S(2)}) async-start(), calls=%async_computation.4 | async-start | bytes 10485760 | tf_op jit(solution)/shard_map/all_gather | solution.py:44
  453.3 262.4 %reduce-scatter.2.cloned.1.call-start = ((), (), s32[]{:S(2)}) async-start(), calls=%async_computation.5 | async-start | bytes 10485760 | tf_op jit(solution)/shard_map/reduce_scatter | solution.py:46
Sparse Core Ops, SparseCore 0:
  20.9 16.3 all-gather.3
  39.2 88.6 all-gather.5
  159.1 290.8 all-reduce.1
  453.4 86.4 all-gather.7
  571.1 144.6 reduce-scatter.1
where the time goes:
time: 728 us; the launch traced here: 727 us
  waiting for transfers between devices  576 us (79%)
  matrix products  62.1 us (9%)
  local copies, waits for them, and re-layouts  61.9 us (9%)
  other arithmetic  13.8 us (2%)
  between operations  13.2 us (2%)
    psum x1, waiting for transfers between devices, local(): square = lax.psum(partial_value, 'layer')  279 us
    reduce_scatter x1, waiting for transfers between devices, local(): lax.psum_scatter(jnp.dot(left_full, filtered_full, preferred_element_type...  108 us
    all_gather x1, waiting for transfers between devices, local(): lax.all_gather(layer_rows(sparse, layers, level), 'row', axis=0, tiled=True)  90.5 us
    all_gather x1, waiting for transfers between devices, local(): filtered_full = lax.all_gather(filtered, 'row', axis=0, tiled=True)  86.4 us
    mul x6, local copies, waits for them, and re-layouts, local(): matrix.reshape(block_rows, BS, block_cols, BS)  38.8 us
    dot_general x1, matrix products, local(): jnp.dot(left_full, right_full, preferred_element_type=jnp.float32, precis...  31 us
    dot_general x1, matrix products, local(): jnp.dot(left_full, filtered_full, preferred_element_type=jnp.float32, pre...  31 us
  transfers between devices with their start and end apart: 5, of which 5 were waited for; matrix products, arithmetic and copies ran while one was open for 7% of the time, Pallas kernels for 0%

commit v1 on v0

--- a/solution.py
+++ b/solution.py
@@ -30,14 +30,16 @@
     left_full = lax.all_gather(left_local, "col", axis=1, tiled=True)
     right_full = lax.all_gather(layer_rows(sparse, layers, level), "row", axis=0, tiled=True)
     partial_value = jnp.dot(
-        left_full, right_full, preferred_element_type=jnp.float32, precision=lax.Precision.HIGHEST
+        left_full, right_full, preferred_element_type=jnp.float32, precision=lax.Precision.HIGH
     )
     keep_flags = keep.astype(jnp.float32)
     keep_mine = lax.dynamic_index_in_dim(
         keep_flags.reshape(block_rows // layers, layers, block_cols), level, 1, keepdims=False
     )
-    square = lax.psum(partial_value, "layer")
-    mine = layer_rows(square, layers, level)
+    by_layer = partial_value.reshape(block_rows // layers, layers, BS, cols).transpose(1, 0, 2, 3)
+    mine = lax.psum_scatter(
+        by_layer.reshape(rows, cols), "layer", scatter_dimension=0, tiled=True
+    )
     filtered = (
         mine.reshape(block_rows // layers, BS, block_cols, BS) * keep_mine[:, None, :, None]
     ).reshape(rows // layers, cols)
@@ -48,7 +50,7 @@
             left_full,
             filtered_full,
             preferred_element_type=jnp.float32,
-            precision=lax.Precision.HIGHEST,
+            precision=lax.Precision.HIGH,
         ),
         "layer",
         scatter_dimension=0,

time: 728 us -> 560 us (0.77)
  waiting for transfers between devices: 576 us -> 431 us
  matrix products: 62.1 us -> 34.9 us
    psum x1 -> x0, waiting for transfers between devices: 279 us -> none  [local(): square = lax.psum(partial_value, 'layer')]
    reduce_scatter x0 -> x1, waiting for transfers between devices: none -> 133 us  [local(): lax.psum_scatter(by_layer.reshape(rows, cols), 'layer', scatter_dimension...]
    dot_general x1, matrix products: 31 us -> 16.8 us  [local(): jnp.dot(left_full, right_full, preferred_element_type=jnp.float32, precis...]
    dot_general x1, matrix products: 31 us -> 18.1 us  [local(): jnp.dot(left_full, filtered_full, preferred_element_type=jnp.float32, pre...]
  transfers between devices with their start and end apart: 5 -> 5, of which waited for: 5 -> 5; matrix products, arithmetic and copies ran while one was open for 7% -> 9% of each run, Pallas kernels for 0% -> 0%
where the time goes in v1:
time: 560 us; the launch traced here: 559 us
  waiting for transfers between devices  431 us (77%)
  local copies, waits for them, and re-layouts  64 us (11%)
  matrix products  34.9 us (6%)
  other arithmetic  15.4 us (3%)
  between operations  13.2 us (2%)
    reduce_scatter x1, waiting for transfers between devices, local(): lax.psum_scatter(by_layer.reshape(rows, cols), 'layer', scatter_dimension...  133 us
    reduce_scatter x1, waiting for transfers between devices, local(): lax.psum_scatter(jnp.dot(left_full, filtered_full, preferred_element_type...  108 us
    all_gather x1, waiting for transfers between devices, local(): lax.all_gather(layer_rows(sparse, layers, level), 'row', axis=0, tiled=True)  90.5 us
    all_gather x1, waiting for transfers between devices, local(): filtered_full = lax.all_gather(filtered, 'row', axis=0, tiled=True)  88 us
    mul x6, local copies, waits for them, and re-layouts, local(): matrix.reshape(block_rows, BS, block_cols, BS)  38.8 us
    dot_general x1, matrix products, local(): jnp.dot(left_full, filtered_full, preferred_element_type=jnp.float32, pre...  18.1 us
    dot_general x1, matrix products, local(): jnp.dot(left_full, right_full, preferred_element_type=jnp.float32, precis...  16.8 us
    all_gather x1, waiting for transfers between devices, local(): left_full = lax.all_gather(left_local, 'col', axis=1, tiled=True)  12.3 us
  transfers between devices with their start and end apart: 5, of which 5 were waited for; matrix products, arithmetic and copies ran while one was open for 9% of the time, Pallas kernels for 0%

profile of v1, /device:TPU:0, one launch (start us, length us, event | category | flops | bytes accessed | tf_op | source)
XLA Modules:
  0.0 559.1 jit_solution(13502446609699732119)
XLA Ops:
  6.5 0.7 convert_element_type.6
  7.3 9.3 %copy.4 = f32[1024,2048]{0,1:T(8,128)} copy(f32[1024,2048]{1,0:T(8,128)} %param.3) | data formatting | bytes 16777216 | tf_op args[0]
  16.6 0.3 mul.63
  16.9 0.5 mul.64
  17.5 3.3 dynamic-slice_multiply_fusion.1
  20.9 0.3 mul.67
  21.2 0.5 mul.68
  21.8 3.3 dynamic-slice_multiply_fusion
  25.1 12.3 %all-gather.4.cloned.1.call-done = f32[1024,1024]{0,1:T(8,128)} async-done(((f32[1024,512]{0,1:T(8,128)}), f32[1024,1024]{0,1:T(8,128)}) %all-gather.4.cloned.1.call-update) | async-done | bytes 4194320 | tf_op jit(solution)/shard_map/all_gather | solution.py:30
  37.4 90.5 %all-gather.6.cloned.1.call-done = f32[1024,2048]{1,0:T(8,128)} async-done(((f32[256,2048]{1,0:T(8,128)}), f32[1024,2048]{1,0:T(8,128)}) %all-gather.6.cloned.1.call-update) | async-done | bytes 8388624 | tf_op jit(solution)/shard_map/all_gather | solution.py:31
  127.9 16.8 %fusion.2 = f32[1024,2048]{1,0:T(8,128)S(1)} fusion(f32[1024,1024]{0,1:T(8,128)} %all-gather.4.cloned.1.call-done, f32[1024,2048]{1,0:T(8,128)} %all-gather.6.cloned.1.call-done), kind=kOutput, calls=%fused_computation.8 | convolution fusion | flops 12884901888 | bytes 20971520 | tf_op jit(solution)/shard_map/dot_general | solution.py:32
  144.7 3.8 copy.6
  148.6 0.6 copy-done
  149.2 4.4 mul.72
  153.6 6.9 %mul.73 = f32[256,2048]{1,0:T(8,128)S(1)} reshape(f32[8,32,64,32]{3,2,1,0:T(8,128)} %mul.72) | data formatting | bytes 4194304 | tf_op jit(solution)/shard_map/mul | solution.py:44
  160.5 132.8 %reduce-scatter.3.cloned.1.call-done = f32[256,2048]{1,0:T(8,128)} async-done(((f32[1024,2048]{1,0:T(8,128)}), f32[256,2048]{1,0:T(8,128)}) %reduce-scatter.3.cloned.1.call-update) | async-done | bytes 2097168 | tf_op jit(solution)/shard_map/reduce_scatter | solution.py:40
  293.3 3.2 mul.74
  296.5 0.2 reduce-scatter.5.cloned.1.call-start
  296.7 88.0 %all-gather.8.cloned.1.call-done = f32[1024,2048]{1,0:T(8,128)} async-done(((f32[256,2048]{1,0:T(8,128)}), f32[1024,2048]{1,0:T(8,128)}) %all-gather.8.cloned.1.call-update) | async-done | bytes 8388624 | tf_op jit(solution)/shard_map/all_gather | solution.py:46
  384.7 18.1 %fusion.3 = f32[1024,2048]{1,0:T(8,128)} fusion(f32[1024,1024]{0,1:T(8,128)} %all-gather.4.cloned.1.call-done, f32[1024,2048]{1,0:T(8,128)} %all-gather.8.cloned.1.call-done), kind=kOutput, calls=%fused_computation.9 | convolution fusion | flops 12884901888 | bytes 20971520 | tf_op jit(solution)/shard_map/dot_general | solution.py:49
  402.8 11.7 %mul.57 = f32[32,32,64,32]{3,2,1,0:T(8,128)} broadcast(f32[32,64]{1,0:T(8,128)S(1)} %convert_element_type.6), dimensions={0,2} | broadcast | bytes 8396800 | tf_op jit(solution)/shard_map/mul | solution.py:23
  414.5 25.5 %mul.58 = f32[1024,2048]{1,0:T(8,128)} reshape(f32[32,32,64,32]{3,2,1,0:T(8,128)} %mul.57) | data formatting | bytes 16777216 | tf_op jit(solution)/shard_map/mul | solution.py:23
  439.9 107.7 %reduce-scatter.5.cloned.1.call-done = f32[256,2048]{1,0:T(8,128)} async-done(((f32[1024,2048]{1,0:T(8,128)}), f32[256,2048]{1,0:T(8,128)}) %reduce-scatter.5.cloned.1.call-update) | async-done | bytes 2097168 | tf_op jit(solution)/shard_map/reduce_scatter | solution.py:48
  547.6 5.0 fusion.1
  (15 shorter events, 0.4 us)
Async XLA Ops:
  6.5 30.8 %all-gather.4.cloned.1.call-start = ((), (), s32[]{:S(2)}) async-start(), calls=%async_computation.2 | async-start | bytes 6291456 | tf_op jit(solution)/shard_map/all_gather | solution.py:30
  20.8 107.1 %all-gather.6.cloned.1.call-start = ((), (), s32[]{:S(2)}) async-start(), calls=%async_computation.3 | async-start | bytes 10485760 | tf_op jit(solution)/shard_map/all_gather | solution.py:31
  25.1 268.2 %reduce-scatter.3.cloned.1.call-start = ((), (), s32[]{:S(2)}) async-start(), calls=%async_computation.4 | async-start | bytes 10485760 | tf_op jit(solution)/shard_map/reduce_scatter | solution.py:40
  148.5 0.7 copy-start
  148.5 236.2 %all-gather.8.cloned.1.call-start = ((), (), s32[]{:S(2)}) async-start(), calls=%async_computation.5 | async-start | bytes 10485760 | tf_op jit(solution)/shard_map/all_gather | solution.py:46
  296.5 251.1 %reduce-scatter.5.cloned.1.call-start = ((), (), s32[]{:S(2)}) async-start(), calls=%async_computation.6 | async-start | bytes 10485760 | tf_op jit(solution)/shard_map/reduce_scatter | solution.py:48
Sparse Core Ops, SparseCore 0:
  20.9 16.3 all-gather.3
  39.2 88.6 all-gather.5
  148.6 144.6 reduce-scatter.2
  296.6 88.0 all-gather.7
  403.0 144.6 reduce-scatter.4
